TPU v7x, 32 devices: a whole 2x2x4 slice. The times are simulated.
32 devices in a mesh: dp: 4 (over z), tp: 8 (over y, x, core).
Axes of the slice: x: 2, y: 2, z: 4, core: 2. Of those that a mesh axis runs over, the one named last changes fastest.
Arguments:
- layer_input: bfloat16 [8192, 2048], P(('dp', 'tp')), may hold values from -6 to 6
- segments: int32 [4, 2048], P('dp'), may hold values from 0 to 1, as said below
- norm_gains: float32 [2, 2048], replicated, may hold values from 0.25 to 1.75
- norm_biases: float32 [2, 2048], replicated, may hold values from -2 to 2
- w_qkv: bfloat16 [2048, 3, 2048], P(None, None, 'tp'), may hold values from -0.125 to 0.125
- qv_bias: float32 [2, 2048], P(None, 'tp'), may hold values from -2 to 2
- key_bias: float32 [32, 16], P('tp'), may hold values from -3 to 3
- w_out: bfloat16 [2048, 2048], P('tp'), may hold values from -2 to 2
- w_gate_up: bfloat16 [2048, 2, 5632], P(None, None, 'tp'), may hold values from -0.125 to 0.125
- w_down: bfloat16 [5632, 2048], P('tp'), may hold values from -0.078125 to 0.078125
- out_grad: bfloat16 [8192, 2048], P(('dp', 'tp')), may hold values from -6 to 6
Outputs:
- output: float32 [8192, 2048], P(('dp', 'tp'))
- grad_x: float32 [8192, 2048], P(('dp', 'tp'))
- grad_qkv: float32 [2048, 3, 2048], P(None, None, 'tp')
- grad_qv_bias: float32 [2, 2048], P(None, 'tp')
- grad_key_bias: float32 [32, 16], P('tp')
- grad_out: float32 [2048, 2048], P('tp')
- grad_gate_up: float32 [2048, 2, 5632], P(None, None, 'tp')
- grad_down: float32 [5632, 2048], P('tp')
- grad_gains: float32 [2, 2048], P(None, 'tp')
- grad_biases: float32 [2, 2048], P(None, 'tp')
Inputs may be any that keep to these rules, and one draw needn't show every extreme that they name: `segments`: in each group the ids number the documents from 0 and never fall; every document has 1024 tokens or more.
All inputs are finite; a program needn't handle non-finite values.
Results may differ from a plain program's by a relative error of at most 0.023.
Values may be sent and summed in bfloat16 or wider, within the bound.
A program may use at most 256 MiB of HBM per device.

v0:
```python
import math
import jax
import jax.numpy as jnp
from jax import lax
from jax.sharding import PartitionSpec as P

D = 2048
HEAD_DIM = 64
ROT = 16
EPSILON = 1e-05


def norm_forward(values, gain, shift_bias):
    centre = jnp.mean(values, axis=-1, keepdims=True)
    centred = values - centre
    spread = jnp.mean(centred * centred, axis=-1, keepdims=True)
    inverse = lax.rsqrt(spread + EPSILON)
    normed = centred * inverse
    return (normed * gain + shift_bias, normed, inverse)


def norm_backward(grad_normed, normed, inverse, gain):
    scaled = grad_normed * gain
    inner = jnp.mean(scaled, axis=-1, keepdims=True)
    along = jnp.mean(scaled * normed, axis=-1, keepdims=True)
    return (
        inverse * (scaled - inner - normed * along),
        jnp.sum(grad_normed * normed, axis=0),
        jnp.sum(grad_normed, axis=0),
    )


def rotary_tables(segment_ids):
    places = jnp.arange(segment_ids.shape[0], dtype=jnp.int32)
    starts_here = jnp.concatenate(
        [jnp.ones((1,), dtype=jnp.bool_), segment_ids[1:] != segment_ids[:-1]]
    )
    doc_start = lax.cummax(jnp.where(starts_here, places, 0), axis=0)
    positions = (places - doc_start).astype(jnp.float32)
    halves = ROT // 2
    frequency = jnp.exp(jnp.arange(halves, dtype=jnp.float32) * (-2.0 * math.log(10000.0) / ROT))
    angles = positions[:, None] * frequency[None, :]
    return (jnp.cos(angles)[:, None, :], jnp.sin(angles)[:, None, :])


def rotate(tensor, cosine, sine):
    halves = ROT // 2
    first_half = tensor[..., :halves]
    second_half = tensor[..., halves:ROT]
    return jnp.concatenate(
        [
            first_half * cosine - second_half * sine,
            second_half * cosine + first_half * sine,
            tensor[..., ROT:],
        ],
        axis=-1,
    )


def rotate_back(tensor, cosine, sine):
    halves = ROT // 2
    first_half = tensor[..., :halves]
    second_half = tensor[..., halves:ROT]
    return jnp.concatenate(
        [
            first_half * cosine + second_half * sine,
            second_half * cosine - first_half * sine,
            tensor[..., ROT:],
        ],
        axis=-1,
    )


def contract_rows(left, right):
    return lax.dot_general(
        left, right, (((0,), (0,)), ((), ())), preferred_element_type=jnp.float32
    )


def contract_cols(left, right):
    return lax.dot_general(
        left, right, (((1,), (1,)), ((), ())), preferred_element_type=jnp.float32
    )


def local(
    layer_input,
    segments,
    norm_gains,
    norm_biases,
    w_qkv,
    qv_bias,
    key_bias,
    w_out,
    w_gate_up,
    w_down,
    out_grad,
):
    segment_ids = segments[0]
    group_rows = segment_ids.shape[0]
    local_width = w_qkv.shape[2]
    local_heads = local_width // HEAD_DIM
    local_hidden = w_down.shape[0]
    block_rows = min(512, group_rows)
    blocks = group_rows // block_rows
    scale = HEAD_DIM ** (-0.5)
    places = jnp.arange(group_rows, dtype=jnp.int32)
    cosine, sine = rotary_tables(segment_ids)
    qkv_matrix = w_qkv.reshape(D, 3 * local_width)
    gate_matrix = w_gate_up.reshape(D, 2 * local_hidden)
    x_float = layer_input.astype(jnp.float32)
    normed_one, hat_one, inverse_one = norm_forward(x_float, norm_gains[0], norm_biases[0])
    rows_one = lax.all_gather(normed_one.astype(jnp.bfloat16), "tp", axis=0, tiled=True)
    projected = jnp.dot(rows_one, qkv_matrix, preferred_element_type=jnp.float32).reshape(
        group_rows, 3, local_heads, HEAD_DIM
    )
    key_full = jnp.concatenate(
        [key_bias, jnp.zeros((local_heads, HEAD_DIM - ROT), jnp.float32)], axis=1
    )
    bias_all = jnp.stack(
        [
            qv_bias[0].reshape(local_heads, HEAD_DIM),
            key_full,
            qv_bias[1].reshape(local_heads, HEAD_DIM),
        ]
    )
    projected = projected + bias_all[None]
    queries = rotate(projected[:, 0], cosine, sine).astype(jnp.bfloat16)
    key_rows = rotate(projected[:, 1], cosine, sine).astype(jnp.bfloat16)
    value_rows = projected[:, 2].astype(jnp.bfloat16)
    query_blocks = queries.reshape(blocks, block_rows, local_heads, HEAD_DIM)
    segment_blocks = segment_ids.reshape(blocks, block_rows)
    place_blocks = places.reshape(blocks, block_rows)

    def scores_of(query_block, segment_block, place_block):
        raw = (
            jnp.einsum("bhd,khd->hbk", query_block, key_rows, preferred_element_type=jnp.float32)
            * scale
        )
        visible = (segment_block[:, None] == segment_ids[None, :]) & (
            place_block[:, None] >= places[None, :]
        )
        return jnp.where(visible[None], raw, -jnp.inf)

    def forward_block(item):
        query_block, segment_block, place_block = item
        scores = scores_of(query_block, segment_block, place_block)
        highest = jnp.max(scores, axis=-1, keepdims=True)
        expo = jnp.exp(scores - highest)
        totals = jnp.sum(expo, axis=-1, keepdims=True)
        probs = (expo / totals).astype(jnp.bfloat16)
        mixed = jnp.einsum("hbk,khd->bhd", probs, value_rows, preferred_element_type=jnp.float32)
        return (mixed.astype(jnp.bfloat16), (highest + jnp.log(totals))[..., 0])

    attended, log_totals = lax.map(forward_block, (query_blocks, segment_blocks, place_blocks))
    attended = attended.reshape(group_rows, local_width)
    hidden_state = x_float + lax.psum_scatter(
        jnp.dot(attended, w_out, preferred_element_type=jnp.float32).astype(jnp.bfloat16),
        "tp",
        scatter_dimension=0,
        tiled=True,
    ).astype(jnp.float32)
    normed_two, hat_two, inverse_two = norm_forward(hidden_state, norm_gains[1], norm_biases[1])
    rows_two = lax.all_gather(normed_two.astype(jnp.bfloat16), "tp", axis=0, tiled=True)
    gate_up = jnp.dot(rows_two, gate_matrix, preferred_element_type=jnp.float32).reshape(
        group_rows, 2, local_hidden
    )
    gate_part = gate_up[:, 0]
    up_part = gate_up[:, 1]
    sigmoid_gate = jax.nn.sigmoid(gate_part)
    silu_gate = gate_part * sigmoid_gate
    activation = (silu_gate * up_part).astype(jnp.bfloat16)
    output = hidden_state + lax.psum_scatter(
        jnp.dot(activation, w_down, preferred_element_type=jnp.float32).astype(jnp.bfloat16),
        "tp",
        scatter_dimension=0,
        tiled=True,
    ).astype(jnp.float32)
    grad_float = out_grad.astype(jnp.float32)
    portion = lax.all_gather(out_grad, "tp", axis=0, tiled=True)
    weight_sum = contract_rows(activation, portion)
    grad_act = contract_cols(portion, w_down)
    grad_down, grad_act = (weight_sum, grad_act)
    grad_gate = grad_act * up_part * sigmoid_gate * (1.0 + gate_part * (1.0 - sigmoid_gate))
    grad_up = grad_act * silu_gate
    grad_pair = (
        jnp.stack([grad_gate, grad_up], axis=1)
        .astype(jnp.bfloat16)
        .reshape(group_rows, 2 * local_hidden)
    )
    grad_gate_up = contract_rows(rows_two, grad_pair).reshape(D, 2, local_hidden)
    grad_normed_two = lax.psum_scatter(
        contract_cols(grad_pair, gate_matrix).astype(jnp.bfloat16),
        "tp",
        scatter_dimension=0,
        tiled=True,
    ).astype(jnp.float32)
    back_two, gain_two, shift_two = norm_backward(
        grad_normed_two, hat_two, inverse_two, norm_gains[1]
    )
    grad_hidden = grad_float + back_two
    portion = lax.all_gather(grad_hidden.astype(jnp.bfloat16), "tp", axis=0, tiled=True)
    weight_sum = contract_rows(attended, portion)
    grad_att = contract_cols(portion, w_out)
    grad_out = weight_sum
    grad_blocks = grad_att.astype(jnp.bfloat16).reshape(blocks, block_rows, local_heads, HEAD_DIM)

    def backward_block(running, item):
        grad_keys, grad_values = running
        query_block, grad_block, log_block, segment_block, place_block = item
        scores = scores_of(query_block, segment_block, place_block)
        weights = jnp.exp(scores - log_block[..., None])
        grad_values = grad_values + jnp.einsum(
            "hbk,bhd->khd",
            weights.astype(jnp.bfloat16),
            grad_block,
            preferred_element_type=jnp.float32,
        )
        grad_weights = jnp.einsum(
            "bhd,khd->hbk", grad_block, value_rows, preferred_element_type=jnp.float32
        )
        inner = jnp.sum(weights * grad_weights, axis=-1, keepdims=True)
        grad_scores = (weights * (grad_weights - inner)).astype(jnp.bfloat16)
        grad_query = (
            jnp.einsum("hbk,khd->bhd", grad_scores, key_rows, preferred_element_type=jnp.float32)
            * scale
        )
        grad_keys = (
            grad_keys
            + jnp.einsum(
                "hbk,bhd->khd", grad_scores, query_block, preferred_element_type=jnp.float32
            )
            * scale
        )
        return ((grad_keys, grad_values), grad_query)

    zero_heads = jnp.zeros((group_rows, local_heads, HEAD_DIM), jnp.float32)
    (grad_keys, grad_values), grad_queries = lax.scan(
        backward_block,
        (zero_heads, zero_heads),
        (query_blocks, grad_blocks, log_totals, segment_blocks, place_blocks),
    )
    grad_queries = grad_queries.reshape(group_rows, local_heads, HEAD_DIM)
    grad_projected = jnp.stack(
        [
            rotate_back(grad_queries, cosine, sine),
            rotate_back(grad_keys, cosine, sine),
            grad_values,
        ],
        axis=1,
    ).astype(jnp.bfloat16)
    bias_sums = jnp.sum(grad_projected, axis=0, dtype=jnp.float32)
    grad_qv = jnp.stack([bias_sums[0].reshape(local_width), bias_sums[2].reshape(local_width)])
    grad_key = bias_sums[1][:, :ROT]
    grad_flat = grad_projected.reshape(group_rows, 3 * local_width)
    grad_qkv = contract_rows(rows_one, grad_flat).reshape(D, 3, local_width)
    grad_normed_one = lax.psum_scatter(
        contract_cols(grad_flat, qkv_matrix).astype(jnp.bfloat16),
        "tp",
        scatter_dimension=0,
        tiled=True,
    ).astype(jnp.float32)
    back_one, gain_one, shift_one = norm_backward(
        grad_normed_one, hat_one, inverse_one, norm_gains[0]
    )
    grad_input = grad_hidden + back_one
    gain_grads, shift_grads = (
        lax.psum_scatter(
            jnp.stack([gain_one, gain_two]).astype(jnp.bfloat16),
            "tp",
            scatter_dimension=1,
            tiled=True,
        ).astype(jnp.float32),
        lax.psum_scatter(
            jnp.stack([shift_one, shift_two]).astype(jnp.bfloat16),
            "tp",
            scatter_dimension=1,
            tiled=True,
        ).astype(jnp.float32),
    )
    grad_qkv, grad_qv, grad_key, grad_out, grad_gate_up, grad_down, gain_grads, shift_grads = (
        lax.psum(grad_qkv.astype(jnp.bfloat16), "dp").astype(jnp.float32),
        lax.psum(grad_qv.astype(jnp.bfloat16), "dp").astype(jnp.float32),
        lax.psum(grad_key.astype(jnp.bfloat16), "dp").astype(jnp.float32),
        lax.psum(grad_out.astype(jnp.bfloat16), "dp").astype(jnp.float32),
        lax.psum(grad_gate_up.astype(jnp.bfloat16), "dp").astype(jnp.float32),
        lax.psum(grad_down.astype(jnp.bfloat16), "dp").astype(jnp.float32),
        lax.psum(gain_grads.astype(jnp.bfloat16), "dp").astype(jnp.float32),
        lax.psum(shift_grads.astype(jnp.bfloat16), "dp").astype(jnp.float32),
    )
    return (
        output,
        grad_input,
        grad_qkv,
        grad_qv,
        grad_key,
        grad_out,
        grad_gate_up,
        grad_down,
        gain_grads,
        shift_grads,
    )


def solution(mesh):
    in_specs = (
        P(("dp", "tp"), None),
        P("dp", None),
        P(),
        P(),
        P(None, None, "tp"),
        P(None, "tp"),
        P("tp", None),
        P("tp", None),
        P(None, None, "tp"),
        P("tp", None),
        P(("dp", "tp"), None),
    )
    out_specs = (
        P(("dp", "tp"), None),
        P(("dp", "tp"), None),
        P(None, None, "tp"),
        P(None, "tp"),
        P("tp", None),
        P("tp", None),
        P(None, None, "tp"),
        P("tp", None),
        P(None, "tp"),
        P(None, "tp"),
    )
    return jax.shard_map(local, mesh=mesh, in_specs=in_specs, out_specs=out_specs, check_vma=False)
```

profile of v0, /device:TPU:0, one launch (start us, length us, event | category | flops | bytes accessed | tf_op | source)
XLA Modules:
  0.0 1480.7 jit_solution(10848038059797148822)
XLA Ops:
  23.3 49.9 %all-gather.5.cloned.1.call-done = bf16[2048,2048]{1,0:T(8,128)(2,1)} async-done(((bf16[256,2048]{1,0:T(8,128)(2,1)}), bf16[2048,2048]{1,0:T(8,128)(2,1)}) %all-gather.5.cloned.1.call-update) | async-done | bytes 8388624 | tf_op jit(solution)/shard_map/all_gather | solution.py:113
  88.5 63.9 %while.28 = (s32[]{:T(128)}, bf16[4,512,4,64]{1,3,2,0:T(8,128)(2,1)}, f32[4,4,512]{2,1,0:T(4,128)S(1)}, s32[4,512]{1,0:T(4,128)S(1)}, s32[1,2048]{1,0:T(1,128)S(...) while((s32[]{:T(128)}, ...), condition=%wide.region_7.8_spmd.clone, body=%wide.region_4.7_spmd.clone.sunk | while | flops 1127348224 | bytes 61427864 | solution.py:155
  161.7 71.6 %reduce-scatter.11.cloned.1.call-done = bf16[256,2048]{1,0:T(8,128)(2,1)} async-done(((bf16[2048,2048]{1,0:T(8,128)(2,1)}), bf16[256,2048]{1,0:T(8,128)(2,1)}) %reduce-scatter.11.cloned.1.call-update) | async-done | bytes 1048592 | tf_op jit(solution)/shard_map/reduce_scatter | solution.py:157
  239.6 53.8 %all-gather.7.cloned.1.call-done = bf16[2048,2048]{1,0:T(8,128)(2,1)} async-done(((bf16[256,2048]{1,0:T(8,128)(2,1)}), bf16[2048,2048]{1,0:T(8,128)(2,1)}) %all-gather.7.cloned.1.call-update) | async-done | bytes 8388624 | tf_op jit(solution)/shard_map/all_gather | solution.py:164
  293.4 18.8 %fusion.53 = f32[2048,2,704]{0,2,1:T(8,128)} fusion(bf16[2048,2048]{1,0:T(8,128)(2,1)} %all-gather.7.cloned.1.call-done, bf16[2048,2,704]{0,2,1:T(8,128)(2,1)} %param.23), kind=kOutput, calls=%fused_computation.64 | convolution fusion | flops 11811160064 | bytes 25690112 | tf_op jit(solution)/shard_map/dot_general | solution.py:165
  312.2 37.2 %all-gather.9.cloned.1.call-done = bf16[2048,2048]{1,0:T(8,128)(2,1)} async-done(((bf16[256,2048]{1,0:T(8,128)(2,1)}), bf16[2048,2048]{1,0:T(8,128)(2,1)}) %all-gather.9.cloned.1.call-update) | async-done | bytes 8388624 | tf_op jit(solution)/shard_map/all_gather | solution.py:180
  349.4 12.9 multiply_bitcast_fusion.1
  364.9 17.9 %bitcast_convert_fusion = bf16[2048,2048]{1,0:T(8,128)(2,1)} fusion(bf16[2048,2,704]{0,2,1:T(8,128)(2,1)} %param.23, bf16[2048,1,704]{0,2,1:T(8,128)(2,1)S(1)} %get-tuple-element.303, bf16[2048,1,704]{0,2,1:T(8,128)(2,1)S(1)} %get-tuple-element.302), kind=kOutput, calls=%fused_computation.56 | convolution fusion | flops 11818237952 | bytes 19922944 | tf_op jit(solution)/shard_map/dot_general | solution.py:81
  382.8 71.6 %reduce-scatter.15.cloned.1.call-done = bf16[256,2048]{1,0:T(8,128)(2,1)} async-done(((bf16[2048,2048]{1,0:T(8,128)(2,1)}), bf16[256,2048]{1,0:T(8,128)(2,1)}) %reduce-scatter.15.cloned.1.call-update) | async-done | bytes 1048592 | tf_op jit(solution)/shard_map/reduce_scatter | solution.py:192
  461.6 54.3 %all-gather.11.cloned.1.call-done = bf16[2048,2048]{1,0:T(8,128)(2,1)} async-done(((bf16[256,2048]{1,0:T(8,128)(2,1)}), bf16[2048,2048]{1,0:T(8,128)(2,1)}) %all-gather.11.cloned.1.call-update) | async-done | bytes 8388624 | tf_op jit(solution)/shard_map/all_gather | solution.py:202
  531.4 245.9 %while.29 = (s32[]{:T(128)}, f32[2048,4,64]{0,2,1:T(8,128)}, f32[2048,4,64]{0,2,1:T(8,128)}, f32[4,512,4,64]{1,0,3,2:T(4,128)}, bf16[4,512,4,64]{1,3,2,0:T(8,128...) while((s32[]{:T(128)}, f32[2048,4,64]{0,2,1:T(8,128)}, ...), condition=%wide.region_17.18_spmd.clone, body=%wide.region_15.17_spmd.clone.sunk | while | flops 2753165312 | bytes 233386272 | solution.py:238
  549.3 12.8 multiply_reduce_fusion.3
  562.1 12.2 multiply_convert_fusion.3
  581.5 11.1 dynamic_update_slice.22
  610.8 12.8 multiply_reduce_fusion.3
  623.6 12.2 multiply_convert_fusion.3
  643.0 11.1 dynamic_update_slice.22
  672.3 12.8 multiply_reduce_fusion.3
  685.1 12.2 multiply_convert_fusion.3
  704.5 11.1 dynamic_update_slice.22
  733.8 12.8 multiply_reduce_fusion.3
  746.6 12.2 multiply_convert_fusion.3
  766.0 11.1 dynamic_update_slice.22
  813.8 11.4 convolution_convert_fusion.3
  825.2 16.2 %fusion.58 = bf16[2048,2,704]{0,2,1:T(8,128)(2,1)} fusion(bf16[2048,2048]{1,0:T(8,128)(2,1)} %all-gather.7.cloned.1.call-done, bf16[2048,1,704]{0,2,1:T(8,128)(2,1)S(1)} %copy-done.47, bf16[2048,1,704]{0,2,1:T(8,128)(2,1)S(1)} %copy-done.45), kind=kOutput, calls=%fused_computation.79 | convolution fusion | flops 11825577984 | bytes 19922944 | tf_op jit(solution)/shard_map/dot_general | solution.py:75
  842.9 11.6 fusion.66
  854.5 14.9 %reduce-scatter.17.cloned.1.call-done = bf16[256,2048]{1,0:T(8,128)(2,1)} async-done(((bf16[2048,2048]{1,0:T(8,128)(2,1)}), bf16[256,2048]{1,0:T(8,128)(2,1)}) %reduce-scatter.17.cloned.1.call-update) | async-done | bytes 1048592 | tf_op jit(solution)/shard_map/reduce_scatter | solution.py:257
  883.5 61.5 %reduce-scatter.13.cloned.1.call-done = bf16[256,2048]{1,0:T(8,128)(2,1)} async-done(((bf16[2048,2048]{1,0:T(8,128)(2,1)}), bf16[256,2048]{1,0:T(8,128)(2,1)}) %reduce-scatter.13.cloned.1.call-update) | async-done | bytes 1048592 | tf_op jit(solution)/shard_map/reduce_scatter | solution.py:173
  950.3 32.5 %reduce-scatter.19.cloned.1.call-done = bf16[256,2]{1,0:T(8,128)(2,1)} async-done(((bf16[2048,2]{1,0:T(8,128)(2,1)}), bf16[256,2]{1,0:T(8,128)(2,1)}) %reduce-scatter.19.cloned.1.call-update) | async-done | bytes 1040
  983.7 36.2 %reduce-scatter.21.cloned.1.call-done = bf16[256,2]{1,0:T(8,128)(2,1)} async-done(((bf16[2048,2]{1,0:T(8,128)(2,1)}), bf16[256,2]{1,0:T(8,128)(2,1)}) %reduce-scatter.21.cloned.1.call-update) | async-done | bytes 1040
  1020.8 11.9 all-reduce.1
  1035.0 423.0 %all-reduce.5.cloned.1.call-done = (bf16[2048,3,256]{2,0,1:T(8,128)(2,1)}, bf16[256,2048]{1,0:T(8,128)(2,1)}, bf16[2048,2,704]{0,2,1:T(8,128)(2,1)}, bf16[704,2048]{1,0:T(8,128)(2,1)}) async-done(((bf16[2048,3,256]{2,0,1:T(8,128)(2,1)}, bf16[256,2048]{1,0:T(8,128)(2,1)}, bf16[2048,2,704]{0,2,1:T(8,128)(2,1)}, bf16[704,2048]{1,0:T(8,128)(2,1)}), (bf16[2048,3,256]{2,0,1:T(8,128)(2,1)}, ...) | async-done | bytes 12845072 | tf_op jit(solution)/shard_map/psum | solution.py:282
  (303 shorter events, 313.6 us)
Async XLA Ops:
  7.2 342.3 %copy-start = (bf16[704,2048]{1,0:T(8,128)(2,1)S(1)}, bf16[704,2048]{1,0:T(8,128)(2,1)}, u32[]{:S(2)}) copy-start(bf16[704,2048]{1,0:T(8,128)(2,1)} %param.24) | copy-start | bytes 8650756
  7.2 66.0 %all-gather.5.cloned.1.call-start = ((), (), s32[]{:S(2)}) async-start(), calls=%async_computation.6 | async-start | bytes 9437184 | tf_op jit(solution)/shard_map/all_gather | solution.py:113
  16.0 217.2 %reduce-scatter.11.cloned.1.call-start = ((), (), s32[]{:S(2)}) async-start(), calls=%async_computation.7 | async-start | bytes 9437184 | tf_op jit(solution)/shard_map/reduce_scatter | solution.py:157
  23.3 61.6 %copy-start.20 = (f32[2048,8]{0,1:T(8,128)}, f32[2048,8]{0,1:T(8,128)S(1)}, u32[]{:S(2)}) copy-start(f32[2048,8]{0,1:T(8,128)S(1)} %get-tuple-element.324) | copy-start | bytes 196612
  23.3 61.6 %copy-start.22 = (f32[2048,8]{0,1:T(8,128)}, f32[2048,8]{0,1:T(8,128)S(1)}, u32[]{:S(2)}) copy-start(f32[2048,8]{0,1:T(8,128)S(1)} %get-tuple-element.325) | copy-start | bytes 196612
  161.6 75.8 %copy-start.24 = (f32[1,2048]{1,0:T(1,128)S(1)}, f32[1,2048]{1,0:T(1,128)}, u32[]{:S(2)}) copy-start(f32[1,2048]{1,0:T(1,128)} %get-tuple-element.321) | copy-start | bytes 24580
  161.6 75.8 %copy-start.30 = (f32[1,2048]{1,0:T(1,128)S(1)}, f32[1,2048]{1,0:T(1,128)}, u32[]{:S(2)}) copy-start(f32[1,2048]{1,0:T(1,128)} %get-tuple-element.323) | copy-start | bytes 24580
  161.7 131.7 %all-gather.7.cloned.1.call-start = ((), (), s32[]{:S(2)}) async-start(), calls=%async_computation.8 | async-start | bytes 9437184 | tf_op jit(solution)/shard_map/all_gather | solution.py:164
  235.3 222.7 %copy-start.28 = (f32[256]{0:T(256)}, f32[256]{0:T(256)S(1)}, u32[]{:S(2)}) copy-start(f32[256]{0:T(256)S(1)} %broadcast_multiply_fusion.4) | copy-start | bytes 3076
  237.4 220.7 %copy-start.33 = (f32[256]{0:T(256)}, f32[256]{0:T(256)S(1)}, u32[]{:S(2)}) copy-start(f32[256]{0:T(256)S(1)} %add_rsqrt_fusion) | copy-start | bytes 3076
  239.0 110.4 %all-gather.9.cloned.1.call-start = ((), (), s32[]{:S(2)}) async-start(), calls=%async_computation.10 | async-start | bytes 9437184 | tf_op jit(solution)/shard_map/all_gather | solution.py:180
  239.6 214.8 %reduce-scatter.15.cloned.1.call-start = ((), (), s32[]{:S(2)}) async-start(), calls=%async_computation.11 | async-start | bytes 9437184 | tf_op jit(solution)/shard_map/reduce_scatter | solution.py:192
  382.8 133.1 %all-gather.11.cloned.1.call-start = ((), (), s32[]{:S(2)}) async-start(), calls=%async_computation.12 | async-start | bytes 9437184 | tf_op jit(solution)/shard_map/all_gather | solution.py:202
  461.5 407.9 %reduce-scatter.17.cloned.1.call-start = ((), (), s32[]{:S(2)}) async-start(), calls=%async_computation.13 | async-start | bytes 9437184 | tf_op jit(solution)/shard_map/reduce_scatter | solution.py:257
  562.1 12.2 copy-start.2
  623.6 12.2 copy-start.2
  685.1 12.2 copy-start.2
  746.5 12.2 copy-start.2
  797.8 147.2 %reduce-scatter.13.cloned.1.call-start = ((), (), s32[]{:S(2)}) async-start(), calls=%async_computation.9 | async-start | bytes 9437184 | tf_op jit(solution)/shard_map/reduce_scatter | solution.py:173
  813.7 169.1 %reduce-scatter.19.cloned.1.call-start = ((), (), s32[]{:S(2)}) async-start(), calls=%async_computation.14 | async-start | bytes 589824
  813.8 11.4 copy-start.45
  825.2 17.6 %copy-start.37 = (bf16[2048]{0:T(1024)(128)(2,1)S(1)}, bf16[2048]{0:T(1024)(128)(2,1)}, u32[]{:S(2)}) copy-start(bf16[2048]{0:T(1024)(128)(2,1)} %get-tuple-element.234) | copy-start | bytes 12292
  842.9 28.0 %copy-start.27 = (f32[1,2048]{1,0:T(1,128)S(1)}, f32[1,2048]{1,0:T(1,128)}, u32[]{:S(2)}) copy-start(f32[1,2048]{1,0:T(1,128)} %copy-done.26) | copy-start | bytes 24580
  842.9 28.0 %copy-start.32 = (f32[256]{0:T(256)S(1)}, f32[256]{0:T(256)}, u32[]{:S(2)}) copy-start(f32[256]{0:T(256)} %copy-done.31) | copy-start | bytes 3076
  842.9 28.0 %copy-start.36 = (f32[256]{0:T(256)S(1)}, f32[256]{0:T(256)}, u32[]{:S(2)}) copy-start(f32[256]{0:T(256)} %copy-done.35) | copy-start | bytes 3076
  874.5 145.4 %reduce-scatter.21.cloned.1.call-start = ((), (), s32[]{:S(2)}) async-start(), calls=%async_computation.15 | async-start | bytes 589824
  875.6 582.3 %all-reduce.5.cloned.1.call-start = ((), (), s32[]{:S(2)}) async-start(), calls=%async_computation.16 | async-start | bytes 25690112 | tf_op jit(solution)/shard_map/psum | solution.py:282
  883.2 61.7 %copy-start.25 = (f32[1,2048]{1,0:T(1,128)S(1)}, f32[1,2048]{1,0:T(1,128)}, u32[]{:S(2)}) copy-start(f32[1,2048]{1,0:T(1,128)} %get-tuple-element.321) | copy-start | bytes 24580
  883.2 61.7 %copy-start.29 = (f32[256]{0:T(256)S(1)}, f32[256]{0:T(256)}, u32[]{:S(2)}) copy-start(f32[256]{0:T(256)} %copy-done.28) | copy-start | bytes 3076
  883.2 61.7 %copy-start.34 = (f32[256]{0:T(256)S(1)}, f32[256]{0:T(256)}, u32[]{:S(2)}) copy-start(f32[256]{0:T(256)} %copy-done.33) | copy-start | bytes 3076
  883.2 61.7 %copy-start.39 = (f32[256]{0:T(256)S(1)}, f32[256]{0:T(256)}, u32[]{:S(2)}) copy-start(f32[256]{0:T(256)} %copy-done.38) | copy-start | bytes 3076
  883.2 61.7 %copy-start.41 = (f32[256]{0:T(256)S(1)}, f32[256]{0:T(256)}, u32[]{:S(2)}) copy-start(f32[256]{0:T(256)} %copy-done.40) | copy-start | bytes 3076
  (44 other events, 176.5 us)
Sparse Core Ops, SparseCore 0:
  16.2 56.9 all-gather.4
  161.8 71.4 reduce-scatter.10
  239.1 54.2 all-gather.6
  295.1 54.2 all-gather.8
  382.9 71.4 reduce-scatter.14
  461.6 54.2 all-gather.10
  797.9 71.4 reduce-scatter.16
  873.4 71.4 reduce-scatter.12
  948.6 34.1 reduce-scatter.18
  985.7 34.1 reduce-scatter.20
  1023.3 434.5 all-reduce.4
where the time goes:
time: 1490 us; the launch traced here: 1480 us
  waiting for transfers between devices  907 us (61%)
  matrix products  296 us (20%)
  other arithmetic  133 us (9%)
  local copies, waits for them, and re-layouts  116 us (8%)
    psum x1, waiting for transfers between devices, local(): lax.psum(grad_qkv.astype(jnp.bfloat16), 'dp').astype(jnp.float32)  423 us
    reduce_scatter x1, waiting for transfers between devices, local(): lax.psum_scatter(contract_cols(grad_pair, gate_matrix).astype(jnp.bfloat1...  71.6 us
    reduce_scatter x1, waiting for transfers between devices, local(): lax.psum_scatter(jnp.dot(attended, w_out, preferred_element_type=jnp.floa...  71.6 us
    unnamed x13, waiting for transfers between devices  69.3 us
    reduce_scatter x1, waiting for transfers between devices, local(): lax.psum_scatter(jnp.dot(activation, w_down, preferred_element_type=jnp.f...  61.5 us
    all_gather x1, waiting for transfers between devices, local(): lax.all_gather(grad_hidden.astype(jnp.bfloat16), 'tp', axis=0, tiled=True)  54.3 us
    all_gather x1, waiting for transfers between devices, local(): lax.all_gather(normed_two.astype(jnp.bfloat16), 'tp', axis=0, tiled=True)  53.8 us
    dot_general x4, matrix products, backward_block(): jnp.einsum('bhd,khd->hbk', grad_block, value_rows, preferred_element_type...  51.2 us
  transfers between devices with their start and end apart: 11, of which 11 were waited for; matrix products, arithmetic and copies ran while one was open for 7% of the time, Pallas kernels for 0%

commit v1 on v0

--- a/solution.py
+++ b/solution.py
@@ -8,6 +8,23 @@
 HEAD_DIM = 64
 ROT = 16
 EPSILON = 1e-05
+
+
+def laid_out(blocks, dim):
+    blocks = jnp.moveaxis(blocks, 0, dim)
+    lengths = blocks.shape
+    return blocks.reshape(*lengths[:dim], lengths[dim] * lengths[dim + 1], *lengths[dim + 2 :])
+
+
+def doubled(x, axis):
+    size, index = (lax.axis_size(axis), lax.axis_index(axis))
+    blocks, bit = (x[None], 1)
+    while bit < size:
+        theirs = lax.ppermute(blocks, axis, [(i, i ^ bit) for i in range(size)])
+        low = index & bit == 0
+        blocks = jnp.concatenate([jnp.where(low, blocks, theirs), jnp.where(low, theirs, blocks)])
+        bit *= 2
+    return blocks
 
 
 def norm_forward(values, gain, shift_bias):
@@ -161,7 +178,8 @@
         tiled=True,
     ).astype(jnp.float32)
     normed_two, hat_two, inverse_two = norm_forward(hidden_state, norm_gains[1], norm_biases[1])
-    rows_two = lax.all_gather(normed_two.astype(jnp.bfloat16), "tp", axis=0, tiled=True)
+    shard = normed_two.astype(jnp.bfloat16)
+    rows_two = laid_out(doubled(shard, "tp"), 0)
     gate_up = jnp.dot(rows_two, gate_matrix, preferred_element_type=jnp.float32).reshape(
         group_rows, 2, local_hidden
     )

time: 1490 us -> 1600 us (1.074)
  waiting for transfers between devices: 907 us -> 986 us
  other arithmetic: 133 us -> 155 us
    ppermute x0 -> x3, waiting for transfers between devices: none -> 171 us  [doubled(): theirs = lax.ppermute(blocks, axis, [(i, i ^ bit) for i in range(size)])]
    all_gather x1 -> x0, waiting for transfers between devices: 53.8 us -> none  [local(): lax.all_gather(normed_two.astype(jnp.bfloat16), 'tp', axis=0, tiled=True)]
    all_gather x1, waiting for transfers between devices: 37.2 us -> 0.01 us  [local(): portion = lax.all_gather(out_grad, 'tp', axis=0, tiled=True)]
    unnamed x13 -> x12, waiting for transfers between devices: 69.3 us -> 69.5 us
  transfers between devices with their start and end apart: 11 -> 13, of which waited for: 11 -> 12; matrix products, arithmetic and copies ran while one was open for 7% -> 8% of each run, Pallas kernels for 0% -> 0%
where the time goes in v1:
time: 1600 us; the launch traced here: 1590 us
  waiting for transfers between devices  986 us (62%)
  matrix products  296 us (18%)
  other arithmetic  155 us (10%)
  local copies, waits for them, and re-layouts  118 us (7%)
    psum x1, waiting for transfers between devices, local(): lax.psum(grad_qkv.astype(jnp.bfloat16), 'dp').astype(jnp.float32)  423 us
    ppermute x3, waiting for transfers between devices, doubled(): theirs = lax.ppermute(blocks, axis, [(i, i ^ bit) for i in range(size)])  171 us
    reduce_scatter x1, waiting for transfers between devices, local(): lax.psum_scatter(contract_cols(grad_pair, gate_matrix).astype(jnp.bfloat1...  71.6 us
    reduce_scatter x1, waiting for transfers between devices, local(): lax.psum_scatter(jnp.dot(attended, w_out, preferred_element_type=jnp.floa...  70.8 us
    unnamed x12, waiting for transfers between devices  69.5 us
    reduce_scatter x1, waiting for transfers between devices, local(): lax.psum_scatter(jnp.dot(activation, w_down, preferred_element_type=jnp.f...  61.5 us
    all_gather x1, waiting for transfers between devices, local(): lax.all_gather(grad_hidden.astype(jnp.bfloat16), 'tp', axis=0, tiled=True)  54.3 us
    dot_general x4, matrix products, backward_block(): jnp.einsum('bhd,khd->hbk', grad_block, value_rows, preferred_element_type...  51.3 us
  transfers between devices with their start and end apart: 13, of which 12 were waited for; matrix products, arithmetic and copies ran while one was open for 8% of the time, Pallas kernels for 0%

profile of v1, /device:TPU:0, one launch (start us, length us, event | category | flops | bytes accessed | tf_op | source)
XLA Modules:
  0.0 1586.5 jit_solution(4718464232833087498)
XLA Ops:
  23.4 49.8 %all-gather.4.cloned.1.call-done = bf16[2048,2048]{1,0:T(8,128)(2,1)} async-done(((bf16[256,2048]{1,0:T(8,128)(2,1)}), bf16[2048,2048]{1,0:T(8,128)(2,1)}) %all-gather.4.cloned.1.call-update) | async-done | bytes 8388624 | tf_op jit(solution)/shard_map/all_gather | solution.py:130
  88.6 63.9 %while.28 = (s32[]{:T(128)}, bf16[4,512,4,64]{1,3,2,0:T(8,128)(2,1)}, f32[4,4,512]{2,1,0:T(4,128)S(1)}, s32[4,512]{1,0:T(4,128)S(1)}, s32[1,2048]{1,0:T(1,128)S(...) while((s32[]{:T(128)}, ...), condition=%wide.region_7.8_spmd.clone, body=%wide.region_4.7_spmd.clone.sunk | while | flops 1127348224 | bytes 61427864 | solution.py:172
  162.5 70.8 %reduce-scatter.11.cloned.1.call-done = bf16[256,2048]{1,0:T(8,128)(2,1)} async-done(((bf16[2048,2048]{1,0:T(8,128)(2,1)}), bf16[256,2048]{1,0:T(8,128)(2,1)}) %reduce-scatter.11.cloned.1.call-update) | async-done | bytes 1048592 | tf_op jit(solution)/shard_map/reduce_scatter | solution.py:174
  247.9 76.5 %collective-permute-done.1 = bf16[2,256,2048]{2,1,0:T(8,128)(2,1)} collective-permute-done((bf16[2,256,2048]{2,1,0:T(8,128)(2,1)}, bf16[2,256,2048]{2,1,0:T(8,128)(2,1)}, u32[]{:S(2)}, u32[]{:S(2)}) %collective-permute-start.1) | collective-permute-done | bytes 2097184 | tf_op jit(solution)/shard_map/ppermute | solution.py:23
  331.7 91.2 %collective-permute-done.2 = bf16[4,256,2048]{2,1,0:T(8,128)(2,1)} collective-permute-done((bf16[4,256,2048]{2,1,0:T(8,128)(2,1)}, bf16[4,256,2048]{2,1,0:T(8,128)(2,1)}, u32[]{:S(2)}, u32[]{:S(2)}) %collective-permute-start.2) | collective-permute-done | bytes 4194336 | tf_op jit(solution)/shard_map/ppermute | solution.py:23
  436.1 18.8 %fusion.53 = f32[2048,2,704]{0,2,1:T(8,128)} fusion(bf16[2048,2048,1]{1,0,2:T(8,128)(2,1)} %bitcast.228, bf16[2048,2,704]{0,2,1:T(8,128)(2,1)} %param.23), kind=kOutput, calls=%fused_computation.71 | convolution fusion | flops 11811160064 | bytes 25690112 | tf_op jit(solution)/shard_map/dot_general | solution.py:183
  454.9 12.9 multiply_bitcast_fusion.1
  470.4 17.9 %bitcast_convert_fusion = bf16[2048,2048]{1,0:T(8,128)(2,1)} fusion(bf16[2048,2,704]{0,2,1:T(8,128)(2,1)} %param.23, bf16[2048,1,704]{0,2,1:T(8,128)(2,1)S(1)} %get-tuple-element.303, bf16[2048,1,704]{0,2,1:T(8,128)(2,1)S(1)} %get-tuple-element.302), kind=kOutput, calls=%fused_computation.56 | convolution fusion | flops 11818237952 | bytes 19922944 | tf_op jit(solution)/shard_map/dot_general | solution.py:98
  488.3 71.6 %reduce-scatter.15.cloned.1.call-done = bf16[256,2048]{1,0:T(8,128)(2,1)} async-done(((bf16[2048,2048]{1,0:T(8,128)(2,1)}), bf16[256,2048]{1,0:T(8,128)(2,1)}) %reduce-scatter.15.cloned.1.call-update) | async-done | bytes 1048592 | tf_op jit(solution)/shard_map/reduce_scatter | solution.py:210
  567.2 54.3 %all-gather.8.cloned.1.call-done = bf16[2048,2048]{1,0:T(8,128)(2,1)} async-done(((bf16[256,2048]{1,0:T(8,128)(2,1)}), bf16[2048,2048]{1,0:T(8,128)(2,1)}) %all-gather.8.cloned.1.call-update) | async-done | bytes 8388624 | tf_op jit(solution)/shard_map/all_gather | solution.py:220
  636.9 246.0 %while.29 = (s32[]{:T(128)}, f32[2048,4,64]{0,2,1:T(8,128)}, f32[2048,4,64]{0,2,1:T(8,128)}, f32[4,512,4,64]{1,0,3,2:T(4,128)}, bf16[4,512,4,64]{1,3,2,0:T(8,128...) while((s32[]{:T(128)}, f32[2048,4,64]{0,2,1:T(8,128)}, ...), condition=%wide.region_17.18_spmd.clone, body=%wide.region_15.17_spmd.clone.sunk | while | flops 2753165312 | bytes 233386272 | solution.py:256
  654.8 12.8 multiply_reduce_fusion.3
  667.6 12.2 multiply_convert_fusion.3
  687.1 11.1 dynamic_update_slice.22
  716.3 12.8 multiply_reduce_fusion.3
  729.1 12.2 multiply_convert_fusion.3
  748.6 11.1 dynamic_update_slice.22
  777.8 12.8 multiply_reduce_fusion.3
  790.6 12.2 multiply_convert_fusion.3
  810.1 11.1 dynamic_update_slice.22
  839.3 12.8 multiply_reduce_fusion.3
  852.1 12.2 multiply_convert_fusion.3
  871.6 11.1 dynamic_update_slice.22
  919.4 11.4 convolution_convert_fusion.3
  930.8 16.2 %fusion.56 = bf16[2048,2,704]{0,2,1:T(8,128)(2,1)} fusion(bf16[2048,2048,1]{1,0,2:T(8,128)(2,1)} %bitcast.229, bf16[2048,1,704]{0,2,1:T(8,128)(2,1)S(1)} %copy-done.51, bf16[2048,1,704]{0,2,1:T(8,128)(2,1)S(1)} %copy-done.49), kind=kOutput, calls=%fused_computation.78 | convolution fusion | flops 11825577984 | bytes 19922944 | tf_op jit(solution)/shard_map/dot_general | solution.py:92
  948.5 11.6 fusion.62
  960.1 14.8 reduce-scatter.17.cloned.1.call-done
  989.0 61.5 %reduce-scatter.13.cloned.1.call-done = bf16[256,2048]{1,0:T(8,128)(2,1)} async-done(((bf16[2048,2048]{1,0:T(8,128)(2,1)}), bf16[256,2048]{1,0:T(8,128)(2,1)}) %reduce-scatter.13.cloned.1.call-update) | async-done | bytes 1048592 | tf_op jit(solution)/shard_map/reduce_scatter | solution.py:191
  1055.9 32.4 %reduce-scatter.19.cloned.1.call-done = bf16[256,2]{1,0:T(8,128)(2,1)} async-done(((bf16[2048,2]{1,0:T(8,128)(2,1)}), bf16[256,2]{1,0:T(8,128)(2,1)}) %reduce-scatter.19.cloned.1.call-update) | async-done | bytes 1040
  1089.2 36.3 %reduce-scatter.21.cloned.1.call-done = bf16[256,2]{1,0:T(8,128)(2,1)} async-done(((bf16[2048,2]{1,0:T(8,128)(2,1)}), bf16[256,2]{1,0:T(8,128)(2,1)}) %reduce-scatter.21.cloned.1.call-update) | async-done | bytes 1040
  1126.4 11.9 all-reduce.1
  1140.6 422.8 %all-reduce.5.cloned.1.call-done = (bf16[2048,3,256]{2,0,1:T(8,128)(2,1)}, bf16[256,2048]{1,0:T(8,128)(2,1)}, bf16[2048,2,704]{0,2,1:T(8,128)(2,1)}, bf16[704,2048]{1,0:T(8,128)(2,1)}) async-done(((bf16[2048,3,256]{2,0,1:T(8,128)(2,1)}, bf16[256,2048]{1,0:T(8,128)(2,1)}, bf16[2048,2,704]{0,2,1:T(8,128)(2,1)}, bf16[704,2048]{1,0:T(8,128)(2,1)}), (bf16[2048,3,256]{2,0,1:T(8,128)(2,1)}, ...) | async-done | bytes 12845072 | tf_op jit(solution)/shard_map/psum | solution.py:300
  (320 shorter events, 343.1 us)
Async XLA Ops:
  7.2 447.7 %copy-start = (bf16[704,2048]{1,0:T(8,128)(2,1)S(1)}, bf16[704,2048]{1,0:T(8,128)(2,1)}, u32[]{:S(2)}) copy-start(bf16[704,2048]{1,0:T(8,128)(2,1)} %param.24) | copy-start | bytes 8650756
  7.2 66.0 %all-gather.4.cloned.1.call-start = ((), (), s32[]{:S(2)}) async-start(), calls=%async_computation.6 | async-start | bytes 9437184 | tf_op jit(solution)/shard_map/all_gather | solution.py:130
  16.0 217.3 %reduce-scatter.11.cloned.1.call-start = ((), (), s32[]{:S(2)}) async-start(), calls=%async_computation.7 | async-start | bytes 9437184 | tf_op jit(solution)/shard_map/reduce_scatter | solution.py:174
  23.4 61.5 %copy-start.24 = (f32[2048,8]{0,1:T(8,128)}, f32[2048,8]{0,1:T(8,128)S(1)}, u32[]{:S(2)}) copy-start(f32[2048,8]{0,1:T(8,128)S(1)} %get-tuple-element.330) | copy-start | bytes 196612
  23.4 61.5 %copy-start.26 = (f32[2048,8]{0,1:T(8,128)}, f32[2048,8]{0,1:T(8,128)S(1)}, u32[]{:S(2)}) copy-start(f32[2048,8]{0,1:T(8,128)S(1)} %get-tuple-element.331) | copy-start | bytes 196612
  161.7 75.8 %copy-start.28 = (f32[1,2048]{1,0:T(1,128)S(1)}, f32[1,2048]{1,0:T(1,128)}, u32[]{:S(2)}) copy-start(f32[1,2048]{1,0:T(1,128)} %get-tuple-element.327) | copy-start | bytes 24580
  161.7 75.8 %copy-start.34 = (f32[1,2048]{1,0:T(1,128)S(1)}, f32[1,2048]{1,0:T(1,128)}, u32[]{:S(2)}) copy-start(f32[1,2048]{1,0:T(1,128)} %get-tuple-element.329) | copy-start | bytes 24580
  161.7 293.2 %all-gather.6.cloned.1.call-start = ((), (), s32[]{:S(2)}) async-start(), calls=%async_computation.9 | async-start | bytes 9437184 | tf_op jit(solution)/shard_map/all_gather | solution.py:198
  162.5 397.5 %reduce-scatter.15.cloned.1.call-start = ((), (), s32[]{:S(2)}) async-start(), calls=%async_computation.10 | async-start | bytes 9437184 | tf_op jit(solution)/shard_map/reduce_scatter | solution.py:210
  235.4 328.2 %copy-start.32 = (f32[256]{0:T(256)}, f32[256]{0:T(256)S(1)}, u32[]{:S(2)}) copy-start(f32[256]{0:T(256)S(1)} %broadcast_multiply_fusion.4) | copy-start | bytes 3076
  237.5 326.2 %copy-start.37 = (f32[256]{0:T(256)}, f32[256]{0:T(256)S(1)}, u32[]{:S(2)}) copy-start(f32[256]{0:T(256)S(1)} %add_rsqrt_fusion) | copy-start | bytes 3076
  239.0 3.0 collective-permute-start
  246.5 78.0 %collective-permute-start.1 = (bf16[2,256,2048]{2,1,0:T(8,128)(2,1)}, bf16[2,256,2048]{2,1,0:T(8,128)(2,1)}, u32[]{:S(2)}, u32[]{:S(2)}) collective-permute-start(bf16[2,256,2048]{2,1,0:T(8,128)(2,1)} %pad_maximum_fusion.2), channel_id=1, source_target_pairs={{0,2},{1,3},{2,0},{3,1},{4,6},{5,7},{6,4},{7,5},{8,10},{9,11},{10,... | collective-permute-start | bytes 6291464 | tf_op jit(solution)/shard_map/ppermute | solution.py:23
  330.2 92.7 %collective-permute-start.2 = (bf16[4,256,2048]{2,1,0:T(8,128)(2,1)}, bf16[4,256,2048]{2,1,0:T(8,128)(2,1)}, u32[]{:S(2)}, u32[]{:S(2)}) collective-permute-start(bf16[4,256,2048]{2,1,0:T(8,128)(2,1)} %pad_maximum_fusion.1), channel_id=1, source_target_pairs={{0,4},{1,5},{2,6},{3,7},{4,0},{5,1},{6,2},{7,3},{8,12},{9,13},{10,... | collective-permute-start | bytes 12582920 | tf_op jit(solution)/shard_map/ppermute | solution.py:23
  488.3 133.2 %all-gather.8.cloned.1.call-start = ((), (), s32[]{:S(2)}) async-start(), calls=%async_computation.11 | async-start | bytes 9437184 | tf_op jit(solution)/shard_map/all_gather | solution.py:220
  567.1 407.9 %reduce-scatter.17.cloned.1.call-start = ((), (), s32[]{:S(2)}) async-start(), calls=%async_computation.12 | async-start | bytes 9437184 | tf_op jit(solution)/shard_map/reduce_scatter | solution.py:275
  729.1 12.2 copy-start.2
  790.6 12.2 copy-start.2
  852.1 12.2 copy-start.2
  903.3 147.2 %reduce-scatter.13.cloned.1.call-start = ((), (), s32[]{:S(2)}) async-start(), calls=%async_computation.8 | async-start | bytes 9437184 | tf_op jit(solution)/shard_map/reduce_scatter | solution.py:191
  919.4 168.9 %reduce-scatter.19.cloned.1.call-start = ((), (), s32[]{:S(2)}) async-start(), calls=%async_computation.13 | async-start | bytes 589824
  930.8 17.6 %copy-start.41 = (bf16[2048]{0:T(1024)(128)(2,1)S(1)}, bf16[2048]{0:T(1024)(128)(2,1)}, u32[]{:S(2)}) copy-start(bf16[2048]{0:T(1024)(128)(2,1)} %get-tuple-element.234) | copy-start | bytes 12292
  948.5 27.9 %copy-start.31 = (f32[1,2048]{1,0:T(1,128)S(1)}, f32[1,2048]{1,0:T(1,128)}, u32[]{:S(2)}) copy-start(f32[1,2048]{1,0:T(1,128)} %copy-done.30) | copy-start | bytes 24580
  948.5 27.9 %copy-start.36 = (f32[256]{0:T(256)S(1)}, f32[256]{0:T(256)}, u32[]{:S(2)}) copy-start(f32[256]{0:T(256)} %copy-done.35) | copy-start | bytes 3076
  948.5 27.9 %copy-start.40 = (f32[256]{0:T(256)S(1)}, f32[256]{0:T(256)}, u32[]{:S(2)}) copy-start(f32[256]{0:T(256)} %copy-done.39) | copy-start | bytes 3076
  980.0 145.5 %reduce-scatter.21.cloned.1.call-start = ((), (), s32[]{:S(2)}) async-start(), calls=%async_computation.14 | async-start | bytes 589824
  981.2 582.2 %all-reduce.5.cloned.1.call-start = ((), (), s32[]{:S(2)}) async-start(), calls=%async_computation.15 | async-start | bytes 25690112 | tf_op jit(solution)/shard_map/psum | solution.py:300
  988.8 61.7 %copy-start.29 = (f32[1,2048]{1,0:T(1,128)S(1)}, f32[1,2048]{1,0:T(1,128)}, u32[]{:S(2)}) copy-start(f32[1,2048]{1,0:T(1,128)} %get-tuple-element.327) | copy-start | bytes 24580
  988.8 61.7 %copy-start.33 = (f32[256]{0:T(256)S(1)}, f32[256]{0:T(256)}, u32[]{:S(2)}) copy-start(f32[256]{0:T(256)} %copy-done.32) | copy-start | bytes 3076
  988.8 61.7 %copy-start.38 = (f32[256]{0:T(256)S(1)}, f32[256]{0:T(256)}, u32[]{:S(2)}) copy-start(f32[256]{0:T(256)} %copy-done.37) | copy-start | bytes 3076
  988.8 61.7 %copy-start.43 = (f32[256]{0:T(256)S(1)}, f32[256]{0:T(256)}, u32[]{:S(2)}) copy-start(f32[256]{0:T(256)} %copy-done.42) | copy-start | bytes 3076
  988.8 61.7 %copy-start.45 = (f32[256]{0:T(256)S(1)}, f32[256]{0:T(256)}, u32[]{:S(2)}) copy-start(f32[256]{0:T(256)} %copy-done.44) | copy-start | bytes 3076
  (50 other events, 209.5 us)
Sparse Core Ops, SparseCore 0:
  16.2 56.9 all-gather.3
  161.8 71.4 reduce-scatter.10
  235.2 83.4 all-gather.5
  488.4 71.5 reduce-scatter.14
  567.2 54.2 all-gather.7
  903.4 71.4 reduce-scatter.16
  979.0 71.4 reduce-scatter.12
  1054.1 34.0 reduce-scatter.18
  1091.4 34.0 reduce-scatter.20
  1128.8 434.5 all-reduce.4
